TPU v7x, 32 devices: a whole 2x2x4 slice. The times are simulated.
32 devices in a mesh: row: 4 (over z), col: 8 (over y, x, core).
Axes of the slice: x: 2, y: 2, z: 4, core: 2. Of those that a mesh axis runs over, the one named last changes fastest.
Arguments:
- minus_gradient: float32 [6, 16384], P(None, ('row', 'col')), may hold values from -10 to 10
- diag_blocks: float32 [36, 16384], P(None, ('row', 'col')), may hold values from -1000 to 1000, as said below
- hess_blocks: float32 [4, 8, 36, 4096], P('row', 'col'), may hold values from -40 to 40, as said below
- block_rows: int32 [4, 8, 4096], P('row', 'col'), may hold values from 0 to 2047
- block_cols: int32 [4, 8, 4096], P('row', 'col'), may hold values from 0 to 4095
- block_counts: int32 [4, 8], P('row', 'col'), may hold values from 0 to 4096, as said below
Outputs:
- pose_update: float32 [6, 16384], P(None, ('row', 'col'))
- residual: float32 [6, 16384], P(None, ('row', 'col'))
Inputs may be any that keep to these rules, and one draw needn't show every extreme that they name: `hess_blocks`: the live blocks of all tiles together with diag_blocks form a symmetric positive definite matrix; no live block lies on the diagonal; the slots after the live ones hold arbitrary entries. `diag_blocks`: each 6x6 block is symmetric positive definite. The live slots of a tile are its first block_counts slots.
All inputs are finite; a program needn't handle non-finite values.
Results may differ from a plain program's by a relative error of at most 0.0003.
Values sent between devices are 32-bit elements; how exact they have to be, the bound alone decides.
No kernel may reach another device: no remote copies, remote signals or barrier semaphores. Data moves between devices by JAX's collectives and lax.ppermute only.
A program may use at most 64 MiB of HBM per device.

v0:
```python
import math
import jax
import jax.numpy as jnp
from jax import lax
from jax.sharding import PartitionSpec as P

ITERS = 3


def factor_blocks(blocks):
    lower_part = {}
    reciprocals = []
    for j in range(6):
        pivot_value = blocks[7 * j]
        for k in range(j):
            pivot_value = pivot_value - lower_part[j, k] * lower_part[j, k]
        reciprocal = 1.0 / jnp.sqrt(pivot_value)
        reciprocals.append(reciprocal)
        for i in range(j + 1, 6):
            entry_value = blocks[6 * i + j]
            for k in range(j):
                entry_value = entry_value - lower_part[i, k] * lower_part[j, k]
            lower_part[i, j] = entry_value * reciprocal
    return (lower_part, reciprocals)


def apply_inverse(lower_part, reciprocals, vector):
    forward = []
    for i in range(6):
        running = vector[i]
        for k in range(i):
            running = running - lower_part[i, k] * forward[k]
        forward.append(running * reciprocals[i])
    backward = [None] * 6
    for i in range(5, -1, -1):
        running = forward[i]
        for k in range(i + 1, 6):
            running = running - lower_part[k, i] * backward[k]
        backward[i] = running * reciprocals[i]
    return jnp.stack(backward)


def diagonal_term(diag_blocks, vector):
    return jnp.sum(diag_blocks.reshape(6, 6, -1) * vector[None], axis=1)


def pick_columns(source, offsets):
    width = source.shape[1]
    low_width = math.gcd(128, width)
    high_width = width // low_width
    table = source.reshape(6 * high_width, low_width)
    slot_count = offsets.shape[0]
    block_size = math.gcd(512, slot_count)
    turns = slot_count // block_size

    def pick_one_block(carry, offset):
        low_part = offset % low_width
        high_part = offset // low_width
        low_onehot = (
            lax.broadcasted_iota(jnp.int32, (low_width, block_size), 0) == low_part[None, :]
        ).astype(jnp.float32)
        spread = jnp.dot(
            table, low_onehot, precision=lax.Precision.HIGHEST, preferred_element_type=jnp.float32
        )
        high_onehot = (
            lax.broadcasted_iota(jnp.int32, (high_width, block_size), 0) == high_part[None, :]
        ).astype(jnp.float32)
        chosen = jnp.sum(spread.reshape(6, high_width, block_size) * high_onehot[None], axis=1)
        return (carry, chosen)

    unused, blocks_out = lax.scan(pick_one_block, None, offsets.reshape(turns, block_size))
    return jnp.transpose(blocks_out, (1, 0, 2)).reshape(6, slot_count)


def add_rows(terms, rows, span_size):
    low_width = math.gcd(128, span_size)
    high_width = span_size // low_width
    slot_count = rows.shape[0]
    block_size = math.gcd(512, slot_count)
    turns = slot_count // block_size
    term_blocks = jnp.transpose(terms.reshape(6, turns, block_size), (1, 0, 2))
    row_blocks = rows.reshape(turns, block_size)

    def add_one_block(carry, inputs):
        term_block, row_block = inputs
        high_onehot = (
            lax.broadcasted_iota(jnp.int32, (high_width, block_size), 0)
            == (row_block // low_width)[None, :]
        ).astype(jnp.float32)
        spread = (term_block[:, None, :] * high_onehot[None]).reshape(6 * high_width, block_size)
        low_onehot = (
            (row_block % low_width)[:, None]
            == lax.broadcasted_iota(jnp.int32, (block_size, low_width), 1)
        ).astype(jnp.float32)
        carry = carry + jnp.dot(
            spread, low_onehot, precision=lax.Precision.HIGHEST, preferred_element_type=jnp.float32
        )
        return (carry, None)

    start_total = jnp.zeros((6 * high_width, low_width), jnp.float32)
    total, unused = lax.scan(add_one_block, start_total, (term_blocks, row_blocks))
    return total.reshape(6, span_size)


def merged_sums(residual, precond, hess_image):
    return lax.psum((jnp.sum(residual * precond), jnp.sum(hess_image * precond)), ("row", "col"))


def on_device(minus_gradient, diag_blocks, hess_blocks, block_rows, block_cols, block_counts):
    pose_dev = minus_gradient.shape[1]
    blocks = hess_blocks.reshape(6, 6, -1)
    local_rows = block_rows.reshape(-1)
    local_cols = block_cols.reshape(-1)
    slot_count = local_rows.shape[0]
    live_mask = jnp.arange(slot_count, dtype=jnp.int32) < block_counts.reshape(())
    span_size = pose_dev * lax.axis_size("row")
    lower_part, reciprocals = factor_blocks(diag_blocks)

    def tile_terms(picked):
        return jnp.sum(blocks * picked[None], axis=1)

    def hessian(vector):
        gathered = lax.all_gather(vector, "col", axis=1, tiled=True)
        picked = pick_columns(gathered, local_cols)
        live_terms = jnp.where(live_mask[None, :], tile_terms(picked), 0.0)
        partial_value = add_rows(live_terms, local_rows, span_size)
        own_term = diagonal_term(diag_blocks, vector)
        summed = lax.psum(partial_value, "row")
        reduced = lax.dynamic_slice_in_dim(summed, lax.axis_index("row") * pose_dev, pose_dev, 1)
        return reduced + own_term

    solution = jnp.zeros_like(minus_gradient)
    residual = minus_gradient
    precond = apply_inverse(lower_part, reciprocals, residual)
    hess_image = hessian(precond)
    rho_now, curv_value = merged_sums(residual, precond, hess_image)
    step_size = rho_now / curv_value
    direction = precond
    along_image = hess_image
    for k in range(ITERS):
        solution = solution + step_size * direction
        residual = residual - step_size * along_image
        if k + 1 < ITERS:
            precond = apply_inverse(lower_part, reciprocals, residual)
            hess_image = hessian(precond)
            rho_next, curv_value = merged_sums(residual, precond, hess_image)
            ratio_next = rho_next / rho_now
            step_size = rho_next / (curv_value - ratio_next * rho_next / step_size)
            direction = precond + ratio_next * direction
            along_image = hess_image + ratio_next * along_image
            rho_now = rho_next
    return (solution, residual)


def solution(mesh):
    placed = (
        P(None, ("row", "col")),
        P(None, ("row", "col")),
        P("row", "col", None, None),
        P("row", "col", None),
        P("row", "col", None),
        P("row", "col"),
    )
    return jax.shard_map(
        on_device,
        mesh=mesh,
        in_specs=placed,
        out_specs=(P(None, ("row", "col")), P(None, ("row", "col"))),
        check_vma=False,
    )
```

profile of v0, /device:TPU:14, one launch (start us, length us, event | category | flops | bytes accessed | tf_op | source)
XLA Modules:
  0.0 246.8 jit_solution(5160269623161957242)
XLA Ops:
  0.6 1.1 subtract_multiply_fusion.21
  1.7 0.7 copy-done.2
  2.6 8.2 %all_gather.9 = f32[6,4096]{1,0:T(8,128)S(1)} all-gather(f32[6,512]{1,0:T(8,128)S(1)} %stack.6), channel_id=1, replica_groups=mesh['row'=4,'col'=8] {'col'}, dimensions={1}, use_global_device_ids=true | all-gather | bytes 110592 | tf_op jit(solution)/shard_map/all_gather | solution.py:123
  10.9 0.5 broadcast.572
  11.5 0.7 reduce.7
  12.3 3.9 %while.75 = (s32[]{:T(128)}, f32[8,6,512]{2,1,0:T(8,128)S(1)}, s32[8,512]{1,0:T(8,128)S(1)}, f32[192,128]{1,0:T(8,128)S(1)}, s32[]{:T(128)}) while((s32[]{:T(128)}, f32[8,6,512]{2,1,0:T(8,128)S(1)}, s32[8,512]{1,0:T(8,128)S(1)}, f32[192,128]{1,0:T(8,128)S(1)}, s32[]{:T(128)}) %tuple.218), condition=%wide.region_4.5_spmd, body=%wide.region_2.4_spmd.sunk | while | flops 151297024 | bytes 1075269 | solution.py:71
  16.2 1.4 reduce
  18.7 0.7 copy-done.4
  19.4 0.7 reduce.8
  20.1 3.9 %while.78 = (s32[]{:T(128)}, f32[96,128]{1,0:T(8,128)S(1)}, f32[8,6,512]{2,1,0:T(8,128)S(1)}, s32[8,512]{1,0:T(8,128)S(1)}, s32[]{:T(128)}, /*index=5*/s32[]{:T(128)}) while((s32[]{:T(128)}, f32[96,128]{1,0:T(8,128)S(1)}, f32[8,6,512]{2,1,0:T(8,128)S(1)}, s32[8,512]{1,0:T(8,128)S(1)}, s32[]{:T(128)}, /*index=5*/s32[]{:T(128)}) %tuple.221), condition=%wide.region_7.8_spmd.clone, body=%wide.region_6.7_spmd.clone.sunk | while | flops 75666432 | bytes 608343 | solution.py:101
  21.6 0.4 convolution_add_fusion.6
  22.6 0.4 convolution_add_fusion.6
  23.6 0.4 convolution_add_fusion.6
  24.0 16.2 %psum.64 = f32[6,2048]{1,0:T(8,128)S(1)} all-reduce(f32[6,2048]{1,0:T(8,128)S(1)} %reshape.316), channel_id=1, replica_groups=mesh['row'=4,'col'=8] {'row'}, use_global_device_ids=true, to_apply=%region_8.9 | all-reduce | flops 12288 | bytes 98304 | tf_op jit(solution)/shard_map/psum | solution.py:128
  40.3 0.6 multiply_reduce_fusion.13
  40.9 44.0 %all-reduce.2 = (f32[]{:T(128)}, f32[]{:T(128)}) all-reduce(f32[]{:T(128)} %get-tuple-element.394, f32[]{:T(128)} %get-tuple-element.393), channel_id=1, replica_groups=mesh['row'=4,'col'=8] {'row','col'}, use_global_device_ids=true, to_apply=%region_1.2 | all-reduce | flops 2 | bytes 16 | tf_op jit(solution)/shard_map/psum | solution.py:106
  86.4 8.2 %all_gather.10 = f32[6,4096]{1,0:T(8,128)S(1)} all-gather(f32[6,512]{1,0:T(8,128)S(1)} %stack.7), channel_id=1, replica_groups=mesh['row'=4,'col'=8] {'col'}, dimensions={1}, use_global_device_ids=true | all-gather | bytes 110592 | tf_op jit(solution)/shard_map/all_gather | solution.py:123
  94.6 3.9 %while.76 = (s32[]{:T(128)}, f32[8,6,512]{2,1,0:T(8,128)S(1)}, s32[8,512]{1,0:T(8,128)S(1)}, f32[192,128]{1,0:T(8,128)S(1)}, s32[]{:T(128)}) while((s32[]{:T(128)}, f32[8,6,512]{2,1,0:T(8,128)S(1)}, s32[8,512]{1,0:T(8,128)S(1)}, f32[192,128]{1,0:T(8,128)S(1)}, s32[]{:T(128)}) %tuple.236), condition=%wide.region_16.17_spmd, body=%wide.region_14.16_spmd.sunk | while | flops 151297024 | bytes 1075269 | solution.py:71
  98.9 3.9 %while.79 = (s32[]{:T(128)}, f32[96,128]{1,0:T(8,128)S(1)}, f32[8,6,512]{2,1,0:T(8,128)S(1)}, s32[8,512]{1,0:T(8,128)S(1)}, s32[]{:T(128)}, /*index=5*/s32[]{:T(128)}) while((s32[]{:T(128)}, f32[96,128]{1,0:T(8,128)S(1)}, f32[8,6,512]{2,1,0:T(8,128)S(1)}, s32[8,512]{1,0:T(8,128)S(1)}, s32[]{:T(128)}, ...), condition=%wide.region_19.20_spmd.clone, body=%wide.region_18.19_spmd.clone.sunk | while | flops 75666432 | bytes 608343 | solution.py:101
  99.5 0.4 convolution_add_fusion.7
  100.5 0.4 convolution_add_fusion.7
  101.4 0.4 convolution_add_fusion.7
  102.8 14.3 %psum.67 = f32[6,2048]{1,0:T(8,128)S(1)} all-reduce(f32[6,2048]{1,0:T(8,128)S(1)} %reshape.319), channel_id=1, replica_groups=mesh['row'=4,'col'=8] {'row'}, use_global_device_ids=true, to_apply=%region_20.21 | all-reduce | flops 12288 | bytes 98304 | tf_op jit(solution)/shard_map/psum | solution.py:128
  117.1 0.7 multiply_reduce_fusion.11
  117.8 44.2 %all-reduce.1 = (f32[]{:T(128)}, f32[]{:T(128)}) all-reduce(f32[]{:T(128)} %get-tuple-element.392, f32[]{:T(128)} %get-tuple-element.391), channel_id=1, replica_groups=mesh['row'=4,'col'=8] {'row','col'}, use_global_device_ids=true, to_apply=%region_13.14 | all-reduce | flops 2 | bytes 16 | tf_op jit(solution)/shard_map/psum | solution.py:106
  166.7 8.1 %all_gather.11 = f32[6,4096]{1,0:T(8,128)S(1)} all-gather(f32[6,512]{1,0:T(8,128)S(1)} %stack.8), channel_id=1, replica_groups=mesh['row'=4,'col'=8] {'col'}, dimensions={1}, use_global_device_ids=true | all-gather | bytes 110592 | tf_op jit(solution)/shard_map/all_gather | solution.py:123
  174.9 3.9 %while.77 = (s32[]{:T(128)}, f32[8,6,512]{2,1,0:T(8,128)S(1)}, s32[8,512]{1,0:T(8,128)S(1)}, f32[192,128]{1,0:T(8,128)S(1)}, s32[]{:T(128)}) while((s32[]{:T(128)}, f32[8,6,512]{2,1,0:T(8,128)S(1)}, s32[8,512]{1,0:T(8,128)S(1)}, f32[192,128]{1,0:T(8,128)S(1)}, s32[]{:T(128)}) %tuple.237), condition=%wide.region_28.29_spmd, body=%wide.region_26.28_spmd.sunk | while | flops 151297024 | bytes 1075269 | solution.py:71
  179.1 3.9 %while.80 = (s32[]{:T(128)}, f32[96,128]{1,0:T(8,128)S(1)}, f32[8,6,512]{2,1,0:T(8,128)S(1)}, s32[8,512]{1,0:T(8,128)S(1)}, s32[]{:T(128)}, /*index=5*/s32[]{:T(128)}) while((s32[]{:T(128)}, f32[96,128]{1,0:T(8,128)S(1)}, f32[8,6,512]{2,1,0:T(8,128)S(1)}, s32[8,512]{1,0:T(8,128)S(1)}, s32[]{:T(128)}, ...), condition=%wide.region_31.32_spmd.clone, body=%wide.region_30.31_spmd.clone.sunk | while | flops 75666432 | bytes 608343 | solution.py:101
  183.0 14.4 %psum.70 = f32[6,2048]{1,0:T(8,128)S(1)} all-reduce(f32[6,2048]{1,0:T(8,128)S(1)} %reshape.321), channel_id=1, replica_groups=mesh['row'=4,'col'=8] {'row'}, use_global_device_ids=true, to_apply=%region_32.33 | all-reduce | flops 12288 | bytes 98304 | tf_op jit(solution)/shard_map/psum | solution.py:128
  197.5 0.6 multiply_reduce_fusion.9
  198.1 44.1 %all-reduce = (f32[]{:T(128)}, f32[]{:T(128)}) all-reduce(f32[]{:T(128)} %get-tuple-element.390, f32[]{:T(128)} %get-tuple-element.389), channel_id=1, replica_groups=mesh['row'=4,'col'=8] {'row','col'}, use_global_device_ids=true, to_apply=%region_25.26 | all-reduce | flops 2 | bytes 16 | tf_op jit(solution)/shard_map/psum | solution.py:106
  246.2 0.6 multiply_subtract_fusion
  (326 shorter events, 20.2 us)
Async XLA Ops:
  0.6 1.1 copy-start.1
  1.7 0.7 copy-start.2
  10.8 0.7 copy-start.3
  12.2 4.0 %copy-start = (f32[1,1,36,4096]{3,1,2,0:T(1,128)S(1)}, f32[1,1,36,4096]{3,1,2,0:T(1,128)}, u32[]{:S(2)}) copy-start(f32[1,1,36,4096]{3,1,2,0:T(1,128)} %param.20) | copy-start | bytes 1769476
  18.6 0.7 copy-start.4
where the time goes:
time: 248 us; the launch traced here: 247 us
  blocking collectives  202 us (81%)
  matrix products  16.6 us (7%)
  between operations  11.5 us (5%)
  other arithmetic  11.1 us (4%)
  loops' own time  2.93 us (1%)
  local copies, waits for them, and re-layouts  2.92 us (1%)
    psum x3, blocking collectives, merged_sums(): lax.psum((jnp.sum(residual * precond), jnp.sum(hess_image * precond)), ('...  132 us
    psum x3, blocking collectives, hessian(): summed = lax.psum(partial_value, 'row')  44.9 us
    all_gather x3, blocking collectives, hessian(): gathered = lax.all_gather(vector, 'col', axis=1, tiled=True)  24.5 us
    dot_general x24, matrix products, add_one_block(): jnp.dot(spread, low_onehot, precision=lax.Precision.HIGHEST, preferred_el...  8.61 us
    dot_general x24, matrix products, pick_one_block(): jnp.dot(table, low_onehot, precision=lax.Precision.HIGHEST, preferred_ele...  7.99 us

commit v1 on v0

--- a/solution.py
+++ b/solution.py
@@ -125,7 +125,8 @@
         live_terms = jnp.where(live_mask[None, :], tile_terms(picked), 0.0)
         partial_value = add_rows(live_terms, local_rows, span_size)
         own_term = diagonal_term(diag_blocks, vector)
-        summed = lax.psum(partial_value, "row")
+        parts = lax.all_gather(partial_value, "row", axis=0, tiled=False)
+        summed = parts.sum(axis=0)
         reduced = lax.dynamic_slice_in_dim(summed, lax.axis_index("row") * pose_dev, pose_dev, 1)
         return reduced + own_term
 

time: 248 us -> 236 us (0.952)
  blocking collectives: 202 us -> 189 us
    psum x3 -> x0, blocking collectives: 44.9 us -> none  [hessian(): summed = lax.psum(partial_value, 'row')]
    all_gather x0 -> x3, blocking collectives: none -> 39 us  [hessian(): parts = lax.all_gather(partial_value, 'row', axis=0, tiled=False)]
    psum x3, blocking collectives: 132 us -> 125 us  [merged_sums(): lax.psum((jnp.sum(residual * precond), jnp.sum(hess_image * precond)), ('...]
where the time goes in v1:
time: 236 us; the launch traced here: 234 us
  blocking collectives  189 us (80%)
  matrix products  16.6 us (7%)
  between operations  11.5 us (5%)
  other arithmetic  11.2 us (5%)
  loops' own time  2.93 us (1%)
  local copies, waits for them, and re-layouts  2.92 us (1%)
    psum x3, blocking collectives, merged_sums(): lax.psum((jnp.sum(residual * precond), jnp.sum(hess_image * precond)), ('...  125 us
    all_gather x3, blocking collectives, hessian(): parts = lax.all_gather(partial_value, 'row', axis=0, tiled=False)  39 us
    all_gather x3, blocking collectives, hessian(): gathered = lax.all_gather(vector, 'col', axis=1, tiled=True)  24.6 us
    dot_general x24, matrix products, add_one_block(): jnp.dot(spread, low_onehot, precision=lax.Precision.HIGHEST, preferred_el...  8.61 us
    dot_general x24, matrix products, pick_one_block(): jnp.dot(table, low_onehot, precision=lax.Precision.HIGHEST, preferred_ele...  7.98 us

profile of v1, /device:TPU:14, one launch (start us, length us, event | category | flops | bytes accessed | tf_op | source)
XLA Modules:
  0.0 234.0 jit_solution(4235402984477237381)
XLA Ops:
  0.6 1.1 subtract_multiply_fusion.21
  1.7 0.7 copy-done.2
  2.6 8.2 %all_gather.18 = f32[6,4096]{1,0:T(8,128)S(1)} all-gather(f32[6,512]{1,0:T(8,128)S(1)} %stack.6), channel_id=1, replica_groups=mesh['row'=4,'col'=8] {'col'}, dimensions={1}, use_global_device_ids=true | all-gather | bytes 110592 | tf_op jit(solution)/shard_map/all_gather | solution.py:123
  10.9 0.5 broadcast.572
  11.5 0.7 reduce.7
  12.3 3.9 %while.75 = (s32[]{:T(128)}, f32[8,6,512]{2,1,0:T(8,128)S(1)}, s32[8,512]{1,0:T(8,128)S(1)}, f32[192,128]{1,0:T(8,128)S(1)}, s32[]{:T(128)}) while((s32[]{:T(128)}, f32[8,6,512]{2,1,0:T(8,128)S(1)}, s32[8,512]{1,0:T(8,128)S(1)}, f32[192,128]{1,0:T(8,128)S(1)}, s32[]{:T(128)}) %tuple.218), condition=%wide.region_4.5_spmd, body=%wide.region_2.4_spmd.sunk | while | flops 151297024 | bytes 1075269 | solution.py:71
  16.2 1.4 reduce
  18.7 0.7 copy-done.4
  19.4 0.7 reduce.8
  20.1 3.9 %while.78 = (s32[]{:T(128)}, f32[96,128]{1,0:T(8,128)S(1)}, f32[8,6,512]{2,1,0:T(8,128)S(1)}, s32[8,512]{1,0:T(8,128)S(1)}, s32[]{:T(128)}, /*index=5*/s32[]{:T(128)}) while((s32[]{:T(128)}, f32[96,128]{1,0:T(8,128)S(1)}, f32[8,6,512]{2,1,0:T(8,128)S(1)}, s32[8,512]{1,0:T(8,128)S(1)}, s32[]{:T(128)}, /*index=5*/s32[]{:T(128)}) %tuple.221), condition=%wide.region_7.8_spmd.clone, body=%wide.region_6.7_spmd.clone.sunk | while | flops 75666432 | bytes 608343 | solution.py:101
  21.6 0.4 convolution_add_fusion.6
  22.6 0.4 convolution_add_fusion.6
  23.6 0.4 convolution_add_fusion.6
  24.0 14.6 %all_gather.19 = f32[4,6,2048]{2,1,0:T(8,128)S(1)} all-gather(f32[1,6,2048]{2,1,0:T(8,128)S(1)} %all_gather_reshape.9), channel_id=1, replica_groups=mesh['row'=4,'col'=8] {'row'}, dimensions={0}, use_global_device_ids=true | all-gather | bytes 245760 | tf_op jit(solution)/shard_map/all_gather | solution.py:128
  38.7 0.6 multiply_reduce_fusion.13
  39.3 41.5 %all-reduce.2 = (f32[]{:T(128)}, f32[]{:T(128)}) all-reduce(f32[]{:T(128)} %get-tuple-element.394, f32[]{:T(128)} %get-tuple-element.393), channel_id=1, replica_groups=mesh['row'=4,'col'=8] {'row','col'}, use_global_device_ids=true, to_apply=%region_1.2 | all-reduce | flops 2 | bytes 16 | tf_op jit(solution)/shard_map/psum | solution.py:106
  82.3 8.2 %all_gather.20 = f32[6,4096]{1,0:T(8,128)S(1)} all-gather(f32[6,512]{1,0:T(8,128)S(1)} %stack.7), channel_id=1, replica_groups=mesh['row'=4,'col'=8] {'col'}, dimensions={1}, use_global_device_ids=true | all-gather | bytes 110592 | tf_op jit(solution)/shard_map/all_gather | solution.py:123
  90.6 3.9 %while.76 = (s32[]{:T(128)}, f32[8,6,512]{2,1,0:T(8,128)S(1)}, s32[8,512]{1,0:T(8,128)S(1)}, f32[192,128]{1,0:T(8,128)S(1)}, s32[]{:T(128)}) while((s32[]{:T(128)}, f32[8,6,512]{2,1,0:T(8,128)S(1)}, s32[8,512]{1,0:T(8,128)S(1)}, f32[192,128]{1,0:T(8,128)S(1)}, s32[]{:T(128)}) %tuple.236), condition=%wide.region_16.17_spmd, body=%wide.region_14.16_spmd.sunk | while | flops 151297024 | bytes 1075269 | solution.py:71
  94.8 3.9 %while.79 = (s32[]{:T(128)}, f32[96,128]{1,0:T(8,128)S(1)}, f32[8,6,512]{2,1,0:T(8,128)S(1)}, s32[8,512]{1,0:T(8,128)S(1)}, s32[]{:T(128)}, /*index=5*/s32[]{:T(128)}) while((s32[]{:T(128)}, f32[96,128]{1,0:T(8,128)S(1)}, f32[8,6,512]{2,1,0:T(8,128)S(1)}, s32[8,512]{1,0:T(8,128)S(1)}, s32[]{:T(128)}, ...), condition=%wide.region_19.20_spmd.clone, body=%wide.region_18.19_spmd.clone.sunk | while | flops 75666432 | bytes 608343 | solution.py:101
  95.9 0.4 convolution_add_fusion.7
  96.9 0.4 convolution_add_fusion.7
  97.8 0.4 convolution_add_fusion.7
  98.7 12.2 %all_gather.21 = f32[4,6,2048]{2,1,0:T(8,128)S(1)} all-gather(f32[1,6,2048]{2,1,0:T(8,128)S(1)} %all_gather_reshape.10), channel_id=1, replica_groups=mesh['row'=4,'col'=8] {'row'}, dimensions={0}, use_global_device_ids=true | all-gather | bytes 245760 | tf_op jit(solution)/shard_map/all_gather | solution.py:128
  111.0 0.7 multiply_reduce_fusion.11
  111.7 42.2 %all-reduce.1 = (f32[]{:T(128)}, f32[]{:T(128)}) all-reduce(f32[]{:T(128)} %get-tuple-element.392, f32[]{:T(128)} %get-tuple-element.391), channel_id=1, replica_groups=mesh['row'=4,'col'=8] {'row','col'}, use_global_device_ids=true, to_apply=%region_13.14 | all-reduce | flops 2 | bytes 16 | tf_op jit(solution)/shard_map/psum | solution.py:106
  158.6 8.2 %all_gather.22 = f32[6,4096]{1,0:T(8,128)S(1)} all-gather(f32[6,512]{1,0:T(8,128)S(1)} %stack.8), channel_id=1, replica_groups=mesh['row'=4,'col'=8] {'col'}, dimensions={1}, use_global_device_ids=true | all-gather | bytes 110592 | tf_op jit(solution)/shard_map/all_gather | solution.py:123
  166.8 3.9 %while.77 = (s32[]{:T(128)}, f32[8,6,512]{2,1,0:T(8,128)S(1)}, s32[8,512]{1,0:T(8,128)S(1)}, f32[192,128]{1,0:T(8,128)S(1)}, s32[]{:T(128)}) while((s32[]{:T(128)}, f32[8,6,512]{2,1,0:T(8,128)S(1)}, s32[8,512]{1,0:T(8,128)S(1)}, f32[192,128]{1,0:T(8,128)S(1)}, s32[]{:T(128)}) %tuple.237), condition=%wide.region_28.29_spmd, body=%wide.region_26.28_spmd.sunk | while | flops 151297024 | bytes 1075269 | solution.py:71
  171.1 3.9 %while.80 = (s32[]{:T(128)}, f32[96,128]{1,0:T(8,128)S(1)}, f32[8,6,512]{2,1,0:T(8,128)S(1)}, s32[8,512]{1,0:T(8,128)S(1)}, s32[]{:T(128)}, /*index=5*/s32[]{:T(128)}) while((s32[]{:T(128)}, f32[96,128]{1,0:T(8,128)S(1)}, f32[8,6,512]{2,1,0:T(8,128)S(1)}, s32[8,512]{1,0:T(8,128)S(1)}, s32[]{:T(128)}, ...), condition=%wide.region_31.32_spmd.clone, body=%wide.region_30.31_spmd.clone.sunk | while | flops 75666432 | bytes 608343 | solution.py:101
  175.0 12.2 %all_gather.23 = f32[4,6,2048]{2,1,0:T(8,128)S(1)} all-gather(f32[1,6,2048]{2,1,0:T(8,128)S(1)} %all_gather_reshape.11), channel_id=1, replica_groups=mesh['row'=4,'col'=8] {'row'}, dimensions={0}, use_global_device_ids=true | all-gather | bytes 245760 | tf_op jit(solution)/shard_map/all_gather | solution.py:128
  187.2 0.6 multiply_reduce_fusion.9
  187.9 41.5 %all-reduce = (f32[]{:T(128)}, f32[]{:T(128)}) all-reduce(f32[]{:T(128)} %get-tuple-element.390, f32[]{:T(128)} %get-tuple-element.389), channel_id=1, replica_groups=mesh['row'=4,'col'=8] {'row','col'}, use_global_device_ids=true, to_apply=%region_25.26 | all-reduce | flops 2 | bytes 16 | tf_op jit(solution)/shard_map/psum | solution.py:106
  233.3 0.6 multiply_subtract_fusion
  (329 shorter events, 20.2 us)
Async XLA Ops:
  0.6 1.1 copy-start.1
  1.7 0.7 copy-start.2
  10.8 0.7 copy-start.3
  12.2 4.0 %copy-start = (f32[1,1,36,4096]{3,1,2,0:T(1,128)S(1)}, f32[1,1,36,4096]{3,1,2,0:T(1,128)}, u32[]{:S(2)}) copy-start(f32[1,1,36,4096]{3,1,2,0:T(1,128)} %param.20) | copy-start | bytes 1769476
  18.6 0.7 copy-start.4
